TPU v7x, 128 devices: a whole 4x4x4 slice. The times are simulated.
128 devices in a mesh: mem: 4 (over z), lat: 32 (over y, x, core).
Axes of the slice: x: 4, y: 4, z: 4, core: 2. Of those that a mesh axis runs over, the one named last changes fastest.
Arguments:
- ensemble: bfloat16 [32, 72, 32, 1440], P('mem', None, 'lat'), may hold values from -6 to 6
- truth: bfloat16 [72, 32, 1440], P(None, 'lat'), may hold values from -6 to 6
- row_weight: float32 [32], P('lat'), may hold values from 0.3 to 7, as said below
Outputs:
- loss: float32 [], replicated
- gradient: bfloat16 [32, 72, 32, 1440], P('mem', None, 'lat')
Inputs may be any that keep to these rules, and one draw needn't show every extreme that they name: `row_weight`: positive.
All inputs are finite; a program needn't handle non-finite values.
Results may differ from a plain program's by a relative error of at most 0.003.
Values may be sent and summed in bfloat16 or wider, within the bound.
A program may use at most 128 MiB of HBM per device.

v0:
```python
import functools

import jax
import jax.numpy as jnp
from jax import lax
from jax.sharding import Mesh
from jax.sharding import PartitionSpec as P

MEM_LAT = ("mem", "lat_0", "lat_1", "lat_2")
LAT = ("lat_0", "lat_1", "lat_2")


def one_axis_at_a_time(array, axes):
    return functools.reduce(lax.psum, axes, array)


def pair_terms(left, right):
    count_left = left.shape[0]
    grouped = left.reshape((count_left // 2, 2) + left.shape[1:])

    def one_group(block):
        diff = block[:, None] - right[None]
        return (jnp.sum(jnp.abs(diff), axis=1), jnp.sum(jnp.sign(diff), axis=1))

    spread, count = lax.map(one_group, grouped)
    return (spread.reshape(left.shape), count.reshape(left.shape))


def finish(values, target, weight, spread, count, members):
    skill = values - target
    cell = jnp.sum(jnp.abs(skill), axis=0) / members - jnp.sum(spread, axis=0) / (
        2.0 * members * (members - 1)
    )
    partial_value = jnp.sum(weight[None, :, None] * cell)
    grad = (weight[None, None, :, None] * (jnp.sign(skill) - count / (members - 1))).astype(
        jnp.bfloat16
    )
    return (partial_value, grad)


def on_device(ensemble, truth, row_weight):
    local_members, channels, rows, cells = ensemble.shape
    groups = lax.axis_size("mem")
    members = local_members * groups
    values = ensemble.astype(jnp.float32)
    spread, count = pair_terms(
        values, lax.all_gather(ensemble, "mem", axis=0, tiled=True).astype(jnp.float32)
    )
    spread, count = (spread, count)
    partial_value, gradient = finish(
        values, truth.astype(jnp.float32)[None], row_weight, spread, count, members
    )
    total = one_axis_at_a_time(partial_value, MEM_LAT)
    loss = total / (channels * rows * lax.axis_size(LAT) * cells)
    return (loss, gradient)


def solution(mesh):
    torus = Mesh(
        mesh.devices.reshape(mesh.shape["mem"], 4, 4, 2), ("mem", "lat_0", "lat_1", "lat_2")
    )
    in_specs = (P("mem", None, LAT, None), P(None, LAT, None), P(LAT))
    out_specs = (P(), P("mem", None, LAT, None))
    return jax.shard_map(
        on_device, mesh=torus, in_specs=in_specs, out_specs=out_specs, check_vma=False
    )
```

profile of v0, /device:TPU:1, one launch (start us, length us, event | category | flops | bytes accessed | tf_op | source)
XLA Modules:
  0.0 206.8 jit_solution(10314588864462379055)
XLA Ops:
  7.2 0.7 all-gather.2.cloned.1.call-update
  7.9 1.9 convert.5
  10.5 1.7 bitcast_convert_fusion.1
  12.3 72.8 %all-gather.2.cloned.1.call-done = bf16[32,72,1,1440]{3,1,2,0:T(8,128)(2,1)} async-done(((bf16[8,72,1,1440]{3,1,2,0:T(8,128)(2,1)}), bf16[32,72,1,1440]{3,1,2,0:T(8,128)(2,1)}) %all-gather.2.cloned.1.call-update) | async-done | bytes 6635536 | tf_op jit(solution)/shard_map/all_gather | solution.py:47
  85.1 10.1 %bitcast_convert_fusion = f32[32,72,1,1440]{3,1,0,2:T(8,128)} fusion(bf16[32,72,1,1440]{3,1,2,0:T(8,128)(2,1)} %all-gather.2.cloned.1.call-done), kind=kLoop, calls=%fused_computation.7 | loop fusion | flops 3317760 | bytes 19906560 | tf_op jit(solution)/shard_map/while | solution.py:25
  95.2 55.2 %while.12 = (s32[]{:T(128)}, f32[4,2,72,1,1440]{4,2,1,3,0:T(8,128)}, f32[4,2,72,1,1440]{4,2,1,3,0:T(8,128)}, f32[4,2,72,1,1440]{4,2,1,3,0:T(8,128)S(1)}, f32[32,72,1,1440]{3,1,0,2:T(8,128)}, /*index=5*/s32[]{:T(128)}) while((s32[]{:T(128)}, f32[4,2,72,1,1440]{4,2,1,3,0:T(8,128)}, f32[4,2,72,1,1440]{4,2,1,3,0:T(8,128)}, ...), condition=%wide.region_4.5_spmd, body=%wide.region_1.4_spmd.sunk | while | flops 32762880 | bytes 20847176 | solution.py:25
  95.2 12.4 %fusion.3 = (f32[2,72,1440]{2,1,0:T(8,128)S(1)}, f32[2,72,1440]{2,1,0:T(8,128)S(1)}) fusion(f32[32,72,1440]{2,1,0:T(8,128)} %bitcast.27, f32[2,72,1440]{2,1,0:T(8,128)S(1)} %dynamic-slice_bitcast_fusion.2), kind=kLoop, calls=%fused_computation.3.clone.1 | loop fusion | flops 32762880 | bytes 15759360 | tf_op jit(solution)/shard_map/while/body/eval_jaxpr/reduce_sum | solution.py:23
  107.6 1.5 bitcast_dynamic-update-slice_fusion.3
  109.1 12.4 %fusion.3 = (f32[2,72,1440]{2,1,0:T(8,128)S(1)}, f32[2,72,1440]{2,1,0:T(8,128)S(1)}) fusion(f32[32,72,1440]{2,1,0:T(8,128)} %bitcast.27, f32[2,72,1440]{2,1,0:T(8,128)S(1)} %dynamic-slice_bitcast_fusion.2), kind=kLoop, calls=%fused_computation.3.clone.1 | loop fusion | flops 32762880 | bytes 15759360 | tf_op jit(solution)/shard_map/while/body/eval_jaxpr/reduce_sum | solution.py:23
  121.5 1.4 bitcast_dynamic-update-slice_fusion.3
  122.9 12.4 %fusion.3 = (f32[2,72,1440]{2,1,0:T(8,128)S(1)}, f32[2,72,1440]{2,1,0:T(8,128)S(1)}) fusion(f32[32,72,1440]{2,1,0:T(8,128)} %bitcast.27, f32[2,72,1440]{2,1,0:T(8,128)S(1)} %dynamic-slice_bitcast_fusion.2), kind=kLoop, calls=%fused_computation.3.clone.1 | loop fusion | flops 32762880 | bytes 15759360 | tf_op jit(solution)/shard_map/while/body/eval_jaxpr/reduce_sum | solution.py:23
  135.3 1.3 bitcast_dynamic-update-slice_fusion.3
  136.7 12.4 %fusion.3 = (f32[2,72,1440]{2,1,0:T(8,128)S(1)}, f32[2,72,1440]{2,1,0:T(8,128)S(1)}) fusion(f32[32,72,1440]{2,1,0:T(8,128)} %bitcast.27, f32[2,72,1440]{2,1,0:T(8,128)S(1)} %dynamic-slice_bitcast_fusion.2), kind=kLoop, calls=%fused_computation.3.clone.1 | loop fusion | flops 32762880 | bytes 15759360 | tf_op jit(solution)/shard_map/while/body/eval_jaxpr/reduce_sum | solution.py:23
  149.1 1.3 bitcast_dynamic-update-slice_fusion.3
  150.4 4.3 %broadcast_multiply_fusion = f32[4,2,72,1,1440]{4,2,1,3,0:T(8,128)} fusion(f32[4,2,72,1,1440]{4,2,1,3,0:T(8,128)} %get-tuple-element.31), kind=kLoop, calls=%fused_computation.10 | loop fusion | flops 829440 | bytes 6635520 | tf_op jit(solution)/shard_map/div | solution.py:35
  154.7 2.4 %reduce_sum.46 = f32[72,1440]{1,0:T(8,128)S(1)} reduce(f32[4,2,72,1,1440]{4,2,1,3,0:T(8,128)} %get-tuple-element.30, f32[]{:T(128)} %constant.15.clone.1), dimensions={0,1,3}, to_apply=%region_5.6 | reduce | flops 725760 | bytes 3732484 | tf_op jit(solution)/shard_map/reduce_sum | solution.py:31
  157.1 0.1 copy-done
  157.2 0.1 copy-done.1
  157.3 4.8 %multiply_convert_fusion = (bf16[8,72,1,1440]{3,1,2,0:T(8,128)(2,1)}, f32[72,1440]{1,0:T(8,128)S(1)}) fusion(f32[8,72,1,1440]{3,1,2,0:T(8,128)} %bitcast.29, f32[]{:T(128)} %bitcast.26, f32[72,1440]{1,0:T(8,128)S(1)} %copy-done.1, bf16[8,72,1,1440]{3,1,2,0:T(8,128)(2,1)S(1)} %copy-done), kind=kLoop, calls=%fused_computation.8 | loop fusion | flops 6531840 | bytes 7464964 | tf_op jit(solution)/shard_map/convert_element_type | solution.py:35
  162.1 0.7 multiply_reduce_fusion
  162.8 7.5 %psum.28 = f32[]{:T(128)} all-reduce(f32[]{:T(128)} %multiply_reduce_fusion), channel_id=1, replica_groups=mesh['mem'=4,'lat_0'=4,'lat_1'=4,'lat_2'=2] {'mem'}, use_global_device_ids=true, to_apply=%region_7.8 | all-reduce | flops 1 | bytes 8 | tf_op jit(solution)/shard_map/psum | solution.py:14
  170.3 9.2 %psum.29 = f32[]{:T(128)} all-reduce(f32[]{:T(128)} %psum.28), channel_id=1, replica_groups=mesh['mem'=4,'lat_0'=4,'lat_1'=4,'lat_2'=2] {'lat_0'}, use_global_device_ids=true, to_apply=%region_8.9 | all-reduce | flops 1 | bytes 8 | tf_op jit(solution)/shard_map/psum | solution.py:14
  179.5 9.0 %psum.30 = f32[]{:T(128)} all-reduce(f32[]{:T(128)} %psum.29), channel_id=1, replica_groups=mesh['mem'=4,'lat_0'=4,'lat_1'=4,'lat_2'=2] {'lat_1'}, use_global_device_ids=true, to_apply=%region_9.10 | all-reduce | flops 1 | bytes 8 | tf_op jit(solution)/shard_map/psum | solution.py:14
  188.5 9.6 %psum.31 = f32[]{:T(128)} all-reduce(f32[]{:T(128)} %psum.30), channel_id=1, replica_groups=mesh['mem'=4,'lat_0'=4,'lat_1'=4,'lat_2'=2] {'lat_2'}, use_global_device_ids=true, to_apply=%region_10.11 | all-reduce | flops 1 | bytes 8 | tf_op jit(solution)/shard_map/psum | solution.py:14
  (9 shorter events, 0.3 us)
Async XLA Ops:
  7.2 77.9 %all-gather.2.cloned.1.call-start = ((), (), s32[]{:S(2)}) async-start(), calls=%async_computation | async-start | bytes 8847360 | tf_op jit(solution)/shard_map/all_gather | solution.py:47
  154.7 2.5 %copy-start = (bf16[8,72,1,1440]{3,1,2,0:T(8,128)(2,1)S(1)}, bf16[8,72,1,1440]{3,1,2,0:T(8,128)(2,1)}, u32[]{:S(2)}) copy-start(bf16[8,72,1,1440]{3,1,2,0:T(8,128)(2,1)} %param.5) | copy-start | bytes 4976644
  154.7 2.6 %copy-start.1 = (f32[72,1440]{1,0:T(8,128)S(1)}, f32[72,1440]{1,0:T(8,128)}, u32[]{:S(2)}) copy-start(f32[72,1440]{1,0:T(8,128)} %bitcast_convert_fusion.1) | copy-start | bytes 1244164
Sparse Core Ops, SparseCore 0:
  9.6 75.4 all-gather.1
where the time goes:
time: 207 us
  other arithmetic  75.4 us (36%)
  waiting for transfers between devices  73.5 us (36%)
  blocking collectives  35.3 us (17%)
  between operations  16.5 us (8%)
  local copies, waits for them, and re-layouts  5.92 us (3%)
    all_gather x1, waiting for transfers between devices, on_device(): lax.all_gather(ensemble, 'mem', axis=0, tiled=True).astype(jnp.float32)  72.8 us
    reduce_sum x4, other arithmetic, one_group(): return (jnp.sum(jnp.abs(diff), axis=1), jnp.sum(jnp.sign(diff), axis=1))  49.4 us
    psum x4, blocking collectives, one_axis_at_a_time(): return functools.reduce(lax.psum, axes, array)  35.3 us
    while x2, other arithmetic, pair_terms(): spread, count = lax.map(one_group, grouped)  12 us
    dynamic_update_slice x4, local copies, waits for them, and re-layouts, pair_terms(): spread, count = lax.map(one_group, grouped)  5.52 us
    convert_element_type x1, other arithmetic, finish(): (weight[None, None, :, None] * (jnp.sign(skill) - count / (members - 1)))...  4.8 us
    div x1, other arithmetic, finish(): count / (members - 1)  4.27 us
  transfers between devices with their start and end apart: 1, of which 1 were waited for; matrix products, arithmetic and copies ran while one was open for 2% of the time, Pallas kernels for 0%

commit v1 on v0

v1 whole, which is shorter than its diff:
```python
import functools

import jax
import jax.numpy as jnp
from jax import lax
from jax.experimental import pallas as pl
from jax.experimental.pallas import tpu as pltpu
from jax.sharding import PartitionSpec as P

MESH = pl.DeviceIdType.MESH
GROUPS = 4
SUB = 8
LANE = 128
CHUNKS = ((0, 512), (512, 512), (1024, 384))
FULL = 1408
EXTRA = 16
SHARE = EXTRA // GROUPS


def sign_of(left, right):
    return jnp.where(left > right, 1.0, jnp.where(left < right, -1.0, 0.0))


def counts_of(x):
    members = x.shape[0]
    count = jnp.zeros_like(x)
    for step in range(1, members // 2 + 1):
        if 2 * step == members:
            s = sign_of(x[:step], x[step:])
            count = count + jnp.concatenate([s, -s], axis=0)
        else:
            s = sign_of(x, jnp.concatenate([x[step:], x[:step]], axis=0))
            count = count + (s - jnp.concatenate([s[-step:], s[:-step]], axis=0))
    return count


def tile_terms(x, t, weight, pairs):
    count = counts_of(x) * (1.0 / pairs)
    skill = jnp.abs(x - t[None])
    cell = jnp.sum(skill - x * count, axis=0)
    grad = weight * (sign_of(x, t[None]) - count)
    return cell, grad.astype(jnp.bfloat16)


def kernel(
    lat_dims, scale, ens, tru, w_ref, out, loss, xin, tin, ex, tex, rv, rex, gv, gex, oex,
    part, stage, load_sem, send_v, recv_v, send_g, recv_g, send_s, recv_s,
):
    me = lax.axis_index("mem")
    lat = lax.axis_index("lat")
    ny, nx, nc = lat_dims
    core = lax.rem(lat, nc)
    x_at = lax.rem(lat // nc, nx)
    y_at = lat // (nc * nx)
    local = ens.shape[0]
    members = local * GROUPS
    rows = ens.shape[1]

    def peer(axis, d):
        if axis == "mem":
            return {"mem": lax.rem(me + d, GROUPS)}
        if axis == "core":
            return {"lat": (y_at * nx + x_at) * nc + lax.rem(core + d, nc)}
        if axis == "x":
            return {"lat": (y_at * nx + lax.rem(x_at + d, nx)) * nc + core}
        return {"lat": (lax.rem(y_at + d, ny) * nx + x_at) * nc + core}

    axes = [("core", nc, core), ("x", nx, x_at), ("y", ny, y_at), ("mem", GROUPS, me)]
    axes = [a for a in axes if a[1] > 1]

    barrier = pltpu.get_barrier_semaphore()
    count = 0
    for axis, size, _ in axes:
        for d in range(1, size):
            pl.semaphore_signal(barrier, inc=1, device_id=peer(axis, d), device_id_type=MESH)
            count += 1
    load_x = pltpu.make_async_copy(ens, xin, load_sem.at[0])
    load_t = pltpu.make_async_copy(tru, tin, load_sem.at[1])
    load_x.start()
    load_t.start()
    load_x.wait()
    load_t.wait()
    pl.semaphore_wait(barrier, count)

    def values_copy(c, d):
        to = lax.rem(me + d, GROUPS)
        if c == len(CHUNKS):
            src, dst = ex.at[:, pl.ds(SHARE * to, SHARE)], rex.at[d - 1]
        else:
            at, wide = CHUNKS[c]
            src = xin.at[:, pl.ds(2 * to, 2), :, pl.ds(at, wide)]
            dst = rv.at[d - 1, :, :, :, pl.ds(at, wide)]
        return pltpu.make_async_remote_copy(
            src_ref=src, dst_ref=dst, send_sem=send_v.at[c, d - 1], recv_sem=recv_v.at[c, d - 1],
            device_id=peer("mem", d), device_id_type=MESH,
        )

    def grads_copy(c, d):
        if c == len(CHUNKS):
            src, dst = gex.at[d - 1], oex.at[:, pl.ds(SHARE * me, SHARE)]
        else:
            at, wide = CHUNKS[c]
            src = gv.at[d - 1, :, :, :, pl.ds(at, wide)]
            dst = out.at[:, pl.ds(2 * me, 2), :, pl.ds(at, wide)]
        return pltpu.make_async_remote_copy(
            src_ref=src, dst_ref=dst, send_sem=send_g.at[c, d - 1], recv_sem=recv_g.at[c, d - 1],
            device_id=peer("mem", GROUPS - d), device_id_type=MESH,
        )

    order = (0, len(CHUNKS)) + tuple(range(1, len(CHUNKS)))
    hops = (2, 1, 3)
    for d in hops:
        values_copy(0, d).start()

    def pack(src, dst):
        for k in range(FULL // LANE):
            dst[k] = src[rows - 1, :, k * LANE : (k + 1) * LANE]
        wide = src.shape[-1] - FULL
        per = LANE // wide
        for g in range(EXTRA - FULL // LANE):
            parts = [
                src[r, :, FULL:].astype(jnp.float32)
                if r < rows
                else jnp.zeros((SUB, wide), jnp.float32)
                for r in range(g * per, (g + 1) * per)
            ]
            dst[FULL // LANE + g] = jnp.concatenate(parts, axis=1).astype(jnp.bfloat16)

    pack(tin, tex)

    @pl.loop(0, local)
    def _(m):
        pack(xin.at[m], ex.at[m])

    for c in order[1:]:
        for d in hops:
            values_copy(c, d).start()

    weight = w_ref[0]
    part[...] = jnp.zeros_like(part)

    def chunk_tiles(c):
        if c == len(CHUNKS):

            def body(k, carry):
                mine = ex[:, SHARE * me + k]
                x = jnp.concatenate([mine] + [rex[d, :, k] for d in range(GROUPS - 1)], axis=0)
                cell, grad = tile_terms(
                    x.astype(jnp.float32), tex[SHARE * me + k].astype(jnp.float32), weight, members - 1
                )
                part[...] += cell
                oex[:, SHARE * me + k] = grad[:local]
                for d in range(GROUPS - 1):
                    gex[d, :, k] = grad[(d + 1) * local : (d + 2) * local]
                return carry

            lax.fori_loop(0, SHARE, body, 0)
        else:
            at, wide = CHUNKS[c]
            tiles = wide // LANE

            def body(k, carry):
                r = k // tiles
                lanes = pl.ds(pl.multiple_of(at + (k - r * tiles) * LANE, LANE), LANE)
                mine = xin[:, 2 * me + r, :, lanes]
                x = jnp.concatenate(
                    [mine] + [rv[d, :, r, :, lanes] for d in range(GROUPS - 1)], axis=0
                )
                cell, grad = tile_terms(
                    x.astype(jnp.float32),
                    tin[2 * me + r, :, lanes].astype(jnp.float32),
                    weight,
                    members - 1,
                )
                part[...] += cell
                out[:, 2 * me + r, :, lanes] = grad[:local]
                for d in range(GROUPS - 1):
                    gv[d, :, r, :, lanes] = grad[(d + 1) * local : (d + 2) * local]
                return carry

            lax.fori_loop(0, 2 * tiles, body, 0)

    for c in order:
        for d in hops:
            values_copy(c, d).wait_recv()
        chunk_tiles(c)
        for d in hops:
            grads_copy(c, d).start()

    part[...] = part[...] * (weight * scale)
    at = 0
    for number, (axis, size, mine) in enumerate(axes):
        copies = []
        for d in range(1, size):
            copies.append(
                pltpu.make_async_remote_copy(
                    src_ref=part.at[number] if False else part,
                    dst_ref=stage.at[number, mine],
                    send_sem=send_s.at[at],
                    recv_sem=recv_s.at[at],
                    device_id=peer(axis, d),
                    device_id_type=MESH,
                )
            )
            at += 1
        for copy in copies:
            copy.start()
        stage[number, mine] = part[...]
        for copy in copies:
            copy.wait()
        total = stage[number, 0]
        for k in range(1, size):
            total = total + stage[number, k]
        part[...] = total
    loss[0, 0] = jnp.sum(part[...])

    for d in hops:
        grads_copy(len(CHUNKS), d).wait_recv()

    @pl.loop(0, local)
    def _(m):
        for k in range(FULL // LANE):
            out[m, rows - 1, :, k * LANE : (k + 1) * LANE] = oex[m, k]
        wide = out.shape[-1] - FULL
        per = LANE // wide
        for g in range(-(-rows // per)):
            tile = oex[m, FULL // LANE + g].astype(jnp.float32)
            for j in range(per):
                if g * per + j < rows:
                    out[m, g * per + j, :, FULL:] = tile[:, j * wide : (j + 1) * wide].astype(
                        jnp.bfloat16
                    )

    for c in range(len(CHUNKS)):
        for d in hops:
            grads_copy(c, d).wait_recv()
    for c in order:
        for d in hops:
            values_copy(c, d).wait_send()
            grads_copy(c, d).wait_send()


def on_device(lat_dims, total_cells, ensemble, truth, row_weight):
    local, channels, _, lon = ensemble.shape
    rows = channels // SUB
    peers = GROUPS - 1
    n_copies = len(CHUNKS) + 1
    bf = jnp.bfloat16
    n_stage = sum(s - 1 for s in lat_dims) + peers
    loss, out = pl.pallas_call(
        functools.partial(
            lambda l, s, e, t, w, o, z, *rest: kernel(l, s, e, t, w, z, o, *rest),
            lat_dims,
            1.0 / (local * GROUPS) / total_cells,
        ),
        out_shape=(
            jax.ShapeDtypeStruct((1, 1), jnp.float32),
            jax.ShapeDtypeStruct((local, rows, SUB, lon), bf),
        ),
        in_specs=[
            pl.BlockSpec(memory_space=pl.ANY),
            pl.BlockSpec(memory_space=pl.ANY),
            pl.BlockSpec(memory_space=pltpu.SMEM),
        ],
        out_specs=(
            pl.BlockSpec(memory_space=pltpu.SMEM),
            pl.BlockSpec(memory_space=pltpu.VMEM),
        ),
        scratch_shapes=[
            pltpu.VMEM((local, rows, SUB, lon), bf),
            pltpu.VMEM((rows, SUB, lon), bf),
            pltpu.VMEM((local, EXTRA, SUB, LANE), bf),
            pltpu.VMEM((EXTRA, SUB, LANE), bf),
            pltpu.VMEM((peers, local, 2, SUB, FULL), bf),
            pltpu.VMEM((peers, local, SHARE, SUB, LANE), bf),
            pltpu.VMEM((peers, local, 2, SUB, FULL), bf),
            pltpu.VMEM((peers, local, SHARE, SUB, LANE), bf),
            pltpu.VMEM((local, EXTRA, SUB, LANE), bf),
            pltpu.VMEM((SUB, LANE), jnp.float32),
            pltpu.VMEM((4, 4, SUB, LANE), jnp.float32),
            pltpu.SemaphoreType.DMA((2,)),
            pltpu.SemaphoreType.DMA((n_copies, peers)),
            pltpu.SemaphoreType.DMA((n_copies, peers)),
            pltpu.SemaphoreType.DMA((n_copies, peers)),
            pltpu.SemaphoreType.DMA((n_copies, peers)),
            pltpu.SemaphoreType.DMA((n_stage,)),
            pltpu.SemaphoreType.DMA((n_stage,)),
        ],
        compiler_params=pltpu.CompilerParams(
            collective_id=0, has_side_effects=True, vmem_limit_bytes=48 * 1024 * 1024
        ),
        name="crps_exchange",
    )(
        ensemble.reshape(local, rows, SUB, lon),
        truth.reshape(rows, SUB, lon),
        row_weight,
    )
    return loss.reshape(()), out.reshape(ensemble.shape)


def solution(mesh, lat_dims=(4, 4, 2)):
    def whole(ensemble, truth, row_weight):
        cells = truth.size
        step = jax.shard_map(
            functools.partial(on_device, lat_dims, cells),
            mesh=mesh,
            in_specs=(P("mem", None, "lat", None), P(None, "lat", None), P("lat")),
            out_specs=(P(), P("mem", None, "lat", None)),
            check_vma=False,
        )
        return step(ensemble, truth, row_weight)

    return whole
```

time: 207 us -> 53.9 us (0.26)
  other arithmetic: 75.4 us -> 0 us
  waiting for transfers between devices: 73.5 us -> 0 us
  Pallas kernels: 0 us -> 47 us
  blocking collectives: 35.3 us -> 0 us
  between operations: 16.5 us -> 3.05 us
  local copies, waits for them, and re-layouts: 5.92 us -> 3.61 us
    all_gather x1 -> x0, waiting for transfers between devices: 72.8 us -> none  [on_device(): lax.all_gather(ensemble, 'mem', axis=0, tiled=True).astype(jnp.float32)]
    reduce_sum x6 -> x0, other arithmetic: 52.6 us -> none  [the longest x4 49.4 us: one_group(): return (jnp.sum(jnp.abs(diff), axis=1), jnp.sum(jnp.sign(diff), axis=1))]
    pallas_call x0 -> x1, Pallas kernels: none -> 47 us  [on_device(): pl.pallas_call(functools.partial(lambda l, s, e, t, w, o, z, *rest: kerne...]
    psum x4 -> x0, blocking collectives: 35.3 us -> none  [one_axis_at_a_time(): return functools.reduce(lax.psum, axes, array)]
    while x2 -> x0, other arithmetic: 12 us -> none  [pair_terms(): spread, count = lax.map(one_group, grouped)]
    dynamic_update_slice x4 -> x0, local copies, waits for them, and re-layouts: 5.52 us -> none  [pair_terms(): spread, count = lax.map(one_group, grouped)]
    convert_element_type x1 -> x0, other arithmetic: 4.8 us -> none  [finish(): (weight[None, None, :, None] * (jnp.sign(skill) - count / (members - 1)))...]
    div x1 -> x0, other arithmetic: 4.27 us -> none  [finish(): count / (members - 1)]
  transfers between devices with their start and end apart: 1 -> 0, of which waited for: 1 -> 0; matrix products, arithmetic and copies ran while one was open for 2% -> 0% of each run, Pallas kernels for 0% -> 0%
where the time goes in v1:
time: 53.9 us; the launch traced here: 53.7 us
  Pallas kernels  47 us (87%)
  local copies, waits for them, and re-layouts  3.61 us (7%)
  between operations  3.05 us (6%)
    pallas_call x1, Pallas kernels, on_device(): pl.pallas_call(functools.partial(lambda l, s, e, t, w, o, z, *rest: kerne...  47 us
    unnamed x5, local copies, waits for them, and re-layouts  3.61 us

profile of v1, /device:TPU:1, one launch (start us, length us, event | category | flops | bytes accessed | tf_op | source)
XLA Modules:
  0.0 53.7 jit_solution(2157270663126708872)
XLA Ops:
  1.3 0.0 copy-start
  1.3 1.5 %copy-done = bf16[8,72,1,1440]{3,1,2,0:T(8,128)(2,1)S(1)} copy-done((bf16[8,72,1,1440]{3,1,2,0:T(8,128)(2,1)S(1)}, bf16[8,72,1,1440]{3,1,2,0:T(8,128)(2,1)}, u32[]{:S(2)}) %copy-start) | copy-done | bytes 1658904
  2.8 0.0 copy-start.1
  2.8 0.9 %copy-done.1 = bf16[72,1,1440]{2,0,1:T(8,128)(2,1)S(1)} copy-done((bf16[72,1,1440]{2,0,1:T(8,128)(2,1)S(1)}, bf16[72,1,1440]{2,0,1:T(8,128)(2,1)}, u32[]{:S(2)}) %copy-start.1) | copy-done | bytes 207384
  3.7 47.0 %crps_exchange.1 = (f32[1,1]{1,0:T(1,128)}, bf16[8,9,8,1440]{3,2,1,0:T(8,128)(2,1)S(1)}) custom-call(bf16[8,9,8,1440]{3,2,1,0:T(8,128)(2,1)S(1)} %bitcast.7, bf16[9,8,1440]{2,1,0:T(8,128)(2,1)S(1)} %bitcast.8, f32[1]{0:T(128)S(6)} %copy.8.w), custom_call_target="tpu_custom_call" | custom-call | tf_op jit(solution)/shard_map/crps_exchange/pallas_call | solution.py:250
  51.4 1.2 %copy.10 = bf16[8,72,1,1440]{3,1,2,0:T(8,128)(2,1)} copy(bf16[8,72,1,1440]{3,1,2,0:T(8,128)(2,1)S(1)} %bitcast.6) | data formatting | bytes 3317760
Async XLA Ops:
  1.3 1.5 %copy-start = (bf16[8,72,1,1440]{3,1,2,0:T(8,128)(2,1)S(1)}, bf16[8,72,1,1440]{3,1,2,0:T(8,128)(2,1)}, u32[]{:S(2)}) copy-start(bf16[8,72,1,1440]{3,1,2,0:T(8,128)(2,1)} %param.3) | copy-start | bytes 4976644
  2.8 0.9 %copy-start.1 = (bf16[72,1,1440]{2,0,1:T(8,128)(2,1)S(1)}, bf16[72,1,1440]{2,0,1:T(8,128)(2,1)}, u32[]{:S(2)}) copy-start(bf16[72,1,1440]{2,0,1:T(8,128)(2,1)} %param.4) | copy-start | bytes 622084

commit v2 on v1

v2 whole, which is shorter than its diff:
```python
import functools

import jax
import jax.numpy as jnp
from jax import lax
from jax.experimental import pallas as pl
from jax.experimental.pallas import tpu as pltpu
from jax.sharding import PartitionSpec as P

MESH = pl.DeviceIdType.MESH
GROUPS = 4
SUB = 8
LANE = 128
CHUNKS = ((0, 512), (512, 384), (896, 384), (1280, 128))
FULL = 1408
DEAL = (3, 4, 3, 4)
EXTRA = sum(DEAL)
FIRST = tuple(sum(DEAL[:rank]) for rank in range(GROUPS))


def sign_of(left, right):
    return jnp.where(left > right, 1.0, jnp.where(left < right, -1.0, 0.0))


def counts_of(x):
    members = x.shape[0]
    count = jnp.zeros_like(x)
    for step in range(1, members // 2 + 1):
        if 2 * step == members:
            s = sign_of(x[:step], x[step:])
            count = count + jnp.concatenate([s, -s], axis=0)
        else:
            s = sign_of(x, jnp.concatenate([x[step:], x[:step]], axis=0))
            count = count + (s - jnp.concatenate([s[-step:], s[:-step]], axis=0))
    return count


def tile_terms(x, t, weight, pairs):
    count = counts_of(x) * (1.0 / pairs)
    skill = jnp.abs(x - t[None])
    cell = jnp.sum(skill - x * count, axis=0)
    grad = weight * (sign_of(x, t[None]) - count)
    return cell, grad.astype(jnp.bfloat16)


def kernel(
    plane, scale, ens, tru, w_hbm, out, loss, xin, tin, ex, tex, rv, rex, gv, gex, oex,
    cells, part, gift, stage, totals, w_ref, load_sem, send_v, recv_v, send_g, recv_g, send_s, recv_s,
    send_t, recv_t, ready,
):
    me = lax.axis_index("mem")
    lat = lax.axis_index("lat")
    local = ens.shape[0]
    members = local * GROUPS
    rows = ens.shape[1]

    def column(d):
        return {"mem": lax.rem(me + d, GROUPS)}

    even = lax.rem(me, 2) == 0
    odd = lax.rem(me, 2) == 1

    barrier = pltpu.get_barrier_semaphore()

    def greet(where):
        pl.semaphore_signal(barrier, inc=1, device_id=where, device_id_type=MESH)

    @pl.when(odd)
    def _():
        greet(column(2))

    @pl.when(even)
    def _():
        for d in (1, 3):
            greet(column(d))

        @pl.loop(1, plane)
        def _(k):
            greet({"lat": lax.rem(lat + k, plane)})

    load_x = pltpu.make_async_copy(ens, xin, load_sem.at[0])
    load_t = pltpu.make_async_copy(tru, tin, load_sem.at[1])
    load_w = pltpu.make_async_copy(w_hbm, w_ref, load_sem.at[2])
    load_w.start()
    load_x.start()
    load_t.start()

    @pl.when(odd)
    def _():
        pl.semaphore_wait(barrier, GROUPS - 1)
        for d in (1, 3):
            pl.semaphore_signal(ready, inc=1, device_id=column(d), device_id_type=MESH)

    @pl.when(even)
    def _():
        pl.semaphore_wait(ready, 2)


    n = len(CHUNKS)

    def remote(src, dst, send, recv, d):
        return pltpu.make_async_remote_copy(
            src_ref=src, dst_ref=dst, send_sem=send, recv_sem=recv,
            device_id=column(d), device_id_type=MESH,
        )

    def values_copy(c, d, owner=None):
        to = lax.rem(me + d, GROUPS)
        if c == n:
            src = ex.at[:, pl.ds(FIRST[owner], DEAL[owner])]
            dst = rex.at[d - 1, :, pl.ds(0, DEAL[owner])]
        else:
            at, wide = CHUNKS[c]
            src = ens.at[:, pl.ds(2 * to, 2), :, pl.ds(at, wide)]
            dst = rv.at[d - 1, :, :, :, pl.ds(at, wide)]
        return remote(src, dst, send_v.at[c, d - 1], recv_v.at[c, d - 1], d)

    def grads_copy(c, d, owner=None):
        if c == n:
            src = gex.at[d - 1, :, pl.ds(0, DEAL[owner])]
            dst = oex.at[:, pl.ds(FIRST[owner], DEAL[owner])]
        else:
            at, wide = CHUNKS[c]
            src = gv.at[d - 1, :, :, :, pl.ds(at, wide)]
            dst = out.at[:, pl.ds(2 * me, 2), :, pl.ds(at, wide)]
        return remote(src, dst, send_g.at[c, d - 1], recv_g.at[c, d - 1], GROUPS - d)

    def one(make, c, d, act, owner):
        if c < n:
            act(make(c, d))
            return
        for rank in range(GROUPS):

            @pl.when(owner == rank)
            def _():
                act(make(c, d, rank))

    def each(make, c, act, to_peer):
        for d in hops:
            one(make, c, d, act, lax.rem(me + d, GROUPS) if to_peer else me)

    order = (0, n) + tuple(range(1, n))

    def send_back(pieces):
        for c, d in pieces:
            one(grads_copy, c, d, lambda copy: copy.start(), me)

    hops = (2, 1, 3)
    start = lambda copy: copy.start()
    landed = lambda copy: copy.wait_recv()
    left = lambda copy: copy.wait_send()
    each(values_copy, 0, start, True)
    load_x.wait()
    load_t.wait()
    load_w.wait()

    def pack(src, dst):
        for k in range(FULL // LANE):
            dst[k] = src[rows - 1, :, k * LANE : (k + 1) * LANE]
        wide = src.shape[-1] - FULL
        per = LANE // wide
        for g in range(EXTRA - FULL // LANE):
            parts = [
                src[r, :, FULL:].astype(jnp.float32)
                if r < rows
                else jnp.zeros((SUB, wide), jnp.float32)
                for r in range(g * per, (g + 1) * per)
            ]
            dst[FULL // LANE + g] = jnp.concatenate(parts, axis=1).astype(jnp.bfloat16)

    pack(tin, tex)

    @pl.loop(0, local)
    def _(m):
        pack(xin.at[m], ex.at[m])

    for c in order[1:-2]:
        each(values_copy, c, start, True)

    def send_values(pieces):
        for c, d in pieces:
            values_copy(c, d).start()

    @pl.when(even)
    def _():
        send_values([(c, d) for c in order[-2:] for d in (1, 3)] + [(c, 2) for c in order[-2:]])

    @pl.when(odd)
    def _():
        send_values([(c, 2) for c in order[-2:]] + [(c, d) for c in order[-2:] for d in (1, 3)])


    weight = w_ref[0]
    cells[...] = jnp.zeros_like(cells)

    def chunk_tiles(c):
        if c == n:
            first, many = FIRST[0], DEAL[0]
            for rank in range(1, GROUPS):
                first = jnp.where(me == rank, FIRST[rank], first)
                many = jnp.where(me == rank, DEAL[rank], many)

            def body(k, carry):
                mine = ex[:, first + k]
                x = jnp.concatenate([mine] + [rex[d, :, k] for d in range(GROUPS - 1)], axis=0)
                cell, grad = tile_terms(
                    x.astype(jnp.float32), tex[first + k].astype(jnp.float32), weight, members - 1
                )
                cells[...] += cell
                oex[:, first + k] = grad[:local]
                for d in range(GROUPS - 1):
                    gex[d, :, k] = grad[(d + 1) * local : (d + 2) * local]
                return carry

            lax.fori_loop(0, many, body, 0)
        else:
            at, wide = CHUNKS[c]
            tiles = wide // LANE

            def body(k, carry):
                r = k // tiles
                lanes = pl.ds(pl.multiple_of(at + (k - r * tiles) * LANE, LANE), LANE)
                mine = xin[:, 2 * me + r, :, lanes]
                x = jnp.concatenate(
                    [mine] + [rv[d, :, r, :, lanes] for d in range(GROUPS - 1)], axis=0
                )
                cell, grad = tile_terms(
                    x.astype(jnp.float32),
                    tin[2 * me + r, :, lanes].astype(jnp.float32),
                    weight,
                    members - 1,
                )
                cells[...] += cell
                out[:, 2 * me + r, :, lanes] = grad[:local]
                for d in range(GROUPS - 1):
                    gv[d, :, r, :, lanes] = grad[(d + 1) * local : (d + 2) * local]
                return carry

            lax.fori_loop(0, 2 * tiles, body, 0)

    for c in order:
        each(values_copy, c, landed, False)
        chunk_tiles(c)

        @pl.when(even)
        def _():
            if c != order[-1]:
                send_back([(c, d) for d in (2, 1, 3)])

        @pl.when(odd)
        def _():
            send_back([(c, d) for d in ((3, 1, 2) if c == 0 else (1, 2))])

    part[...] = jnp.sum(cells[...], axis=0, keepdims=True) * (weight * scale)
    hand = pltpu.make_async_remote_copy(
        src_ref=part, dst_ref=gift, send_sem=send_t.at[0], recv_sem=recv_t.at[0],
        device_id=column(1), device_id_type=MESH,
    )

    def tell(half, d):
        return pltpu.make_async_remote_copy(
            src_ref=part, dst_ref=totals.at[half], send_sem=send_t.at[d],
            recv_sem=recv_t.at[1 + half], device_id=column(d), device_id_type=MESH,
        )

    half = me // 2

    @pl.when(odd)
    def _():
        hand.start()
        send_back([(c, 3) for c in order[1:]])

    @pl.when(even)
    def _():
        pl.semaphore_wait(barrier, plane - 1)
        hand.wait_recv()
        part[...] += gift[...]

        def share(k):
            return pltpu.make_async_remote_copy(
                src_ref=part, dst_ref=stage.at[lat], send_sem=send_s.at[k - 1],
                recv_sem=recv_s.at[k - 1], device_id={"lat": lax.rem(lat + k, plane)},
                device_id_type=MESH,
            )

        @pl.loop(1, plane)
        def _(k):
            share(k).start()

        stage[lat] = part[...]

        @pl.loop(1, plane)
        def _(k):
            share(k).wait()

        part[...] = jnp.sum(stage[...], axis=0)
        for d in hops:
            tell(half, d).start()
        totals[half] = part[...]
        send_back([(order[-1], d) for d in hops])

    each(grads_copy, n, landed, True)

    @pl.loop(0, local)
    def _(m):
        for k in range(FULL // LANE):
            out[m, rows - 1, :, k * LANE : (k + 1) * LANE] = oex[m, k]
        wide = out.shape[-1] - FULL
        per = LANE // wide
        for g in range(-(-rows // per)):
            tile = oex[m, FULL // LANE + g].astype(jnp.float32)
            for j in range(per):
                if g * per + j < rows:
                    out[m, g * per + j, :, FULL:] = tile[:, j * wide : (j + 1) * wide].astype(
                        jnp.bfloat16
                    )

    @pl.when(even)
    def _():
        tell(1 - half, 2).wait_recv()
        for d in hops:
            tell(half, d).wait_send()

    @pl.when(odd)
    def _():
        for k in range(2):
            tell(k, 1).wait_recv()
        hand.wait_send()

    loss[...] = jnp.full(loss.shape, jnp.sum(totals[0] + totals[1]))

    for c in range(n):
        each(grads_copy, c, landed, True)
    for c in order:
        each(values_copy, c, left, True)
        each(grads_copy, c, left, False)


def hand_over(loss, grads, loss_out, grads_out, loss_at, sems):
    copies = [
        pltpu.make_async_copy(grads.at[m], grads_out.at[m], sems.at[m])
        for m in range(grads.shape[0])
    ]
    for copy in copies:
        copy.start()
    loss_at[0] = loss[0, 0]
    last = pltpu.make_async_copy(loss_at, loss_out, sems.at[grads.shape[0]])
    last.start()
    for copy in copies:
        copy.wait()
    last.wait()


def on_device(total_cells, ensemble, truth, row_weight):
    local, channels, _, lon = ensemble.shape
    rows = channels // SUB
    peers = GROUPS - 1
    plane = lax.axis_size("lat")
    n_copies = len(CHUNKS) + 1
    bf = jnp.bfloat16
    loss, out = pl.pallas_call(
        functools.partial(
            lambda l, s, e, t, w, o, z, *rest: kernel(l, s, e, t, w, z, o, *rest),
            plane,
            1.0 / (local * GROUPS) / total_cells,
        ),
        out_shape=(
            jax.ShapeDtypeStruct((1, LANE), jnp.float32),
            jax.ShapeDtypeStruct((local, rows, SUB, lon), bf),
        ),
        in_specs=[
            pl.BlockSpec(memory_space=pl.ANY),
            pl.BlockSpec(memory_space=pl.ANY),
            pl.BlockSpec(memory_space=pltpu.HBM),
        ],
        out_specs=(
            pl.BlockSpec(memory_space=pltpu.VMEM),
            pl.BlockSpec(memory_space=pltpu.VMEM),
        ),
        scratch_shapes=[
            pltpu.VMEM((local, rows, SUB, lon), bf),
            pltpu.VMEM((rows, SUB, lon), bf),
            pltpu.VMEM((local, EXTRA, SUB, LANE), bf),
            pltpu.VMEM((EXTRA, SUB, LANE), bf),
            pltpu.VMEM((peers, local, 2, SUB, FULL), bf),
            pltpu.VMEM((peers, local, max(DEAL), SUB, LANE), bf),
            pltpu.VMEM((peers, local, 2, SUB, FULL), bf),
            pltpu.VMEM((peers, local, max(DEAL), SUB, LANE), bf),
            pltpu.VMEM((local, EXTRA, SUB, LANE), bf),
            pltpu.VMEM((SUB, LANE), jnp.float32),
            pltpu.VMEM((1, LANE), jnp.float32),
            pltpu.VMEM((1, LANE), jnp.float32),
            pltpu.VMEM((plane, 1, LANE), jnp.float32),
            pltpu.VMEM((2, 1, LANE), jnp.float32),
            pltpu.SMEM((1,), jnp.float32),
            pltpu.SemaphoreType.DMA((3,)),
            pltpu.SemaphoreType.DMA((n_copies, peers)),
            pltpu.SemaphoreType.DMA((n_copies, peers)),
            pltpu.SemaphoreType.DMA((n_copies, peers)),
            pltpu.SemaphoreType.DMA((n_copies, peers)),
            pltpu.SemaphoreType.DMA((plane - 1,)),
            pltpu.SemaphoreType.DMA((plane - 1,)),
            pltpu.SemaphoreType.DMA((GROUPS,)),
            pltpu.SemaphoreType.DMA((3,)),
            pltpu.SemaphoreType.REGULAR,
        ],
        compiler_params=pltpu.CompilerParams(
            collective_id=0, has_side_effects=True, vmem_limit_bytes=48 * 1024 * 1024
        ),
        name="crps_exchange",
    )(
        pltpu.with_memory_space_constraint(ensemble.reshape(local, rows, SUB, lon), pltpu.HBM),
        pltpu.with_memory_space_constraint(truth.reshape(rows, SUB, lon), pltpu.HBM),
        row_weight,
    )
    loss, out = pl.pallas_call(
        hand_over,
        out_shape=(
            jax.ShapeDtypeStruct((1,), jnp.float32),
            jax.ShapeDtypeStruct(out.shape, out.dtype),
        ),
        in_specs=[pl.BlockSpec(memory_space=pltpu.VMEM)] * 2,
        out_specs=(pl.BlockSpec(memory_space=pl.ANY), pl.BlockSpec(memory_space=pl.ANY)),
        scratch_shapes=[pltpu.SMEM((1,), jnp.float32), pltpu.SemaphoreType.DMA((local + 1,))],
        compiler_params=pltpu.CompilerParams(vmem_limit_bytes=4 * 1024 * 1024),
        name="hand_over",
    )(loss, out)
    return loss.reshape(()), out.reshape(ensemble.shape)


def solution(mesh):
    def whole(ensemble, truth, row_weight):
        cells = truth.size
        step = jax.shard_map(
            functools.partial(on_device, cells),
            mesh=mesh,
            in_specs=(P("mem", None, "lat", None), P(None, "lat", None), P("lat")),
            out_specs=(P(), P("mem", None, "lat", None)),
            check_vma=False,
        )
        return step(ensemble, truth, row_weight)

    return whole
```

time: 53.9 us -> 47 us (0.87)
  local copies, waits for them, and re-layouts: 3.61 us -> 0 us
  between operations: 3.05 us -> 1.28 us
  Pallas kernels: 47 us -> 45.4 us
    unnamed x5 -> x0, local copies, waits for them, and re-layouts: 3.61 us -> none
    pallas_call x1, Pallas kernels: 47 us -> 44.2 us  [on_device(): pl.pallas_call(functools.partial(lambda l, s, e, t, w, o, z, *rest: kerne...]
    pallas_call x0 -> x1, Pallas kernels: none -> 1.29 us  [on_device(): pl.pallas_call(hand_over, out_shape=(jax.ShapeDtypeStruct((1,), jnp.float...]
where the time goes in v2:
time: 47 us; the launch traced here: 46.7 us
  Pallas kernels  45.4 us (97%)
  between operations  1.28 us (3%)
    pallas_call x1, Pallas kernels, on_device(): pl.pallas_call(functools.partial(lambda l, s, e, t, w, o, z, *rest: kerne...  44.2 us
    pallas_call x1, Pallas kernels, on_device(): pl.pallas_call(hand_over, out_shape=(jax.ShapeDtypeStruct((1,), jnp.float...  1.29 us

profile of v2, /device:TPU:1, one launch (start us, length us, event | category | flops | bytes accessed | tf_op | source)
XLA Modules:
  0.0 46.7 jit_solution(3698396600180175813)
XLA Ops:
  1.3 44.2 %crps_exchange.1 = (f32[1,128]{1,0:T(1,128)S(1)}, bf16[8,9,8,1440]{3,2,1,0:T(8,128)(2,1)S(1)}) custom-call(bf16[8,9,8,1440]{3,2,1,0:T(8,128)(2,1)} %bitcast.6, bf16[9,8,1440]{2,1,0:T(8,128)(2,1)} %bitcast.7, f32[1]{0:T(128)S(6)} %copy.6.w), custom_call_target="tpu_custom_call" | custom-call | tf_op jit(solution)/shard_map/crps_exchange/pallas_call | solution.py:361
  45.4 1.3 %hand_over.1 = (f32[1]{0:T(128)}, bf16[8,9,8,1440]{3,2,1,0:T(8,128)(2,1)}) custom-call(f32[1,128]{1,0:T(1,128)S(1)} %get-tuple-element.6.loss, bf16[8,9,8,1440]{3,2,1,0:T(8,128)(2,1)S(1)} %get-tuple-element.7.grads), custom_call_target="tpu_custom_call" | custom-call | tf_op jit(solution)/shard_map/hand_over/pallas_call | solution.py:416

commit v3 on v2

--- a/solution.py
+++ b/solution.py
@@ -88,12 +88,11 @@
     @pl.when(odd)
     def _():
         pl.semaphore_wait(barrier, GROUPS - 1)
-        for d in (1, 3):
-            pl.semaphore_signal(ready, inc=1, device_id=column(d), device_id_type=MESH)
+        pl.semaphore_signal(ready, inc=1, device_id=column(3), device_id_type=MESH)
 
     @pl.when(even)
     def _():
-        pl.semaphore_wait(ready, 2)
+        pl.semaphore_wait(ready, 1)
 
 
     n = len(CHUNKS)
@@ -111,7 +110,7 @@
             dst = rex.at[d - 1, :, pl.ds(0, DEAL[owner])]
         else:
             at, wide = CHUNKS[c]
-            src = ens.at[:, pl.ds(2 * to, 2), :, pl.ds(at, wide)]
+            src = xin.at[:, pl.ds(2 * to, 2), :, pl.ds(at, wide)]
             dst = rv.at[d - 1, :, :, :, pl.ds(at, wide)]
         return remote(src, dst, send_v.at[c, d - 1], recv_v.at[c, d - 1], d)
 
@@ -149,8 +148,8 @@
     start = lambda copy: copy.start()
     landed = lambda copy: copy.wait_recv()
     left = lambda copy: copy.wait_send()
+    load_x.wait()
     each(values_copy, 0, start, True)
-    load_x.wait()
     load_t.wait()
     load_w.wait()
 
@@ -174,21 +173,8 @@
     def _(m):
         pack(xin.at[m], ex.at[m])
 
-    for c in order[1:-2]:
+    for c in order[1:]:
         each(values_copy, c, start, True)
-
-    def send_values(pieces):
-        for c, d in pieces:
-            values_copy(c, d).start()
-
-    @pl.when(even)
-    def _():
-        send_values([(c, d) for c in order[-2:] for d in (1, 3)] + [(c, 2) for c in order[-2:]])
-
-    @pl.when(odd)
-    def _():
-        send_values([(c, 2) for c in order[-2:]] + [(c, d) for c in order[-2:] for d in (1, 3)])
-
 
     weight = w_ref[0]
     cells[...] = jnp.zeros_like(cells)

time: 47 us -> 46.3 us (0.985)
  Pallas kernels: 45.4 us -> 44.8 us
    pallas_call x1, Pallas kernels: 44.2 us -> 43.5 us  [on_device(): pl.pallas_call(functools.partial(lambda l, s, e, t, w, o, z, *rest: kerne...]
where the time goes in v3:
time: 46.3 us; the launch traced here: 46.1 us
  Pallas kernels  44.8 us (97%)
  between operations  1.28 us (3%)
    pallas_call x1, Pallas kernels, on_device(): pl.pallas_call(functools.partial(lambda l, s, e, t, w, o, z, *rest: kerne...  43.5 us
    pallas_call x1, Pallas kernels, on_device(): pl.pallas_call(hand_over, out_shape=(jax.ShapeDtypeStruct((1,), jnp.float...  1.29 us

profile of v3, /device:TPU:1, one launch (start us, length us, event | category | flops | bytes accessed | tf_op | source)
XLA Modules:
  0.0 46.1 jit_solution(5574880493765132779)
XLA Ops:
  1.3 43.5 %crps_exchange.1 = (f32[1,128]{1,0:T(1,128)S(1)}, bf16[8,9,8,1440]{3,2,1,0:T(8,128)(2,1)S(1)}) custom-call(bf16[8,9,8,1440]{3,2,1,0:T(8,128)(2,1)} %bitcast.6, bf16[9,8,1440]{2,1,0:T(8,128)(2,1)} %bitcast.7, f32[1]{0:T(128)S(6)} %copy.6.w), custom_call_target="tpu_custom_call" | custom-call | tf_op jit(solution)/shard_map/crps_exchange/pallas_call | solution.py:347
  44.8 1.3 %hand_over.1 = (f32[1]{0:T(128)}, bf16[8,9,8,1440]{3,2,1,0:T(8,128)(2,1)}) custom-call(f32[1,128]{1,0:T(1,128)S(1)} %get-tuple-element.6.loss, bf16[8,9,8,1440]{3,2,1,0:T(8,128)(2,1)S(1)} %get-tuple-element.7.grads), custom_call_target="tpu_custom_call" | custom-call | tf_op jit(solution)/shard_map/hand_over/pallas_call | solution.py:402

commit v4 on v3

--- a/solution.py
+++ b/solution.py
@@ -18,8 +18,13 @@
 FIRST = tuple(sum(DEAL[:rank]) for rank in range(GROUPS))
 
 
+def spread_out(x):
+    tiny = jnp.minimum(jnp.maximum(x, -(2.0**-113)), 2.0**-113)
+    return tiny * 2.0**66 * 2.0**67 + x * 2.0**124
+
+
 def sign_of(left, right):
-    return jnp.where(left > right, 1.0, jnp.where(left < right, -1.0, 0.0))
+    return jnp.minimum(jnp.maximum(left - right, -1.0), 1.0)
 
 
 def counts_of(x):
@@ -36,10 +41,11 @@
 
 
 def tile_terms(x, t, weight, pairs):
-    count = counts_of(x) * (1.0 / pairs)
+    place = spread_out(x)
+    count = counts_of(place) * (1.0 / pairs)
     skill = jnp.abs(x - t[None])
     cell = jnp.sum(skill - x * count, axis=0)
-    grad = weight * (sign_of(x, t[None]) - count)
+    grad = weight * (sign_of(place, spread_out(t)[None]) - count)
     return cell, grad.astype(jnp.bfloat16)
 
 

time: 46.3 us -> 46.1 us (level)
  no operation moved by 1% of the time
where the time goes in v4:
time: 46.1 us; the launch traced here: 45.9 us
  Pallas kernels  44.7 us (97%)
  between operations  1.28 us (3%)
    pallas_call x1, Pallas kernels, on_device(): pl.pallas_call(functools.partial(lambda l, s, e, t, w, o, z, *rest: kerne...  43.4 us
    pallas_call x1, Pallas kernels, on_device(): pl.pallas_call(hand_over, out_shape=(jax.ShapeDtypeStruct((1,), jnp.float...  1.29 us

profile of v4, /device:TPU:1, one launch (start us, length us, event | category | flops | bytes accessed | tf_op | source)
XLA Modules:
  0.0 45.9 jit_solution(16831665455189880340)
XLA Ops:
  1.3 43.4 %crps_exchange.1 = (f32[1,128]{1,0:T(1,128)S(1)}, bf16[8,9,8,1440]{3,2,1,0:T(8,128)(2,1)S(1)}) custom-call(bf16[8,9,8,1440]{3,2,1,0:T(8,128)(2,1)} %bitcast.6, bf16[9,8,1440]{2,1,0:T(8,128)(2,1)} %bitcast.7, f32[1]{0:T(128)S(6)} %copy.6.w), custom_call_target="tpu_custom_call" | custom-call | tf_op jit(solution)/shard_map/crps_exchange/pallas_call | solution.py:353
  44.7 1.3 %hand_over.1 = (f32[1]{0:T(128)}, bf16[8,9,8,1440]{3,2,1,0:T(8,128)(2,1)}) custom-call(f32[1,128]{1,0:T(1,128)S(1)} %get-tuple-element.6.loss, bf16[8,9,8,1440]{3,2,1,0:T(8,128)(2,1)S(1)} %get-tuple-element.7.grads), custom_call_target="tpu_custom_call" | custom-call | tf_op jit(solution)/shard_map/hand_over/pallas_call | solution.py:408

commit v5 on v4

--- a/solution.py
+++ b/solution.py
@@ -150,7 +150,7 @@
         for c, d in pieces:
             one(grads_copy, c, d, lambda copy: copy.start(), me)
 
-    hops = (2, 1, 3)
+    hops = (2, 3, 1)
     start = lambda copy: copy.start()
     landed = lambda copy: copy.wait_recv()
     left = lambda copy: copy.wait_send()

time: 46.1 us -> 46.1 us (level)
  no operation moved by 1% of the time
where the time goes in v5:
time: 46.1 us; the launch traced here: 45.9 us
  Pallas kernels  44.7 us (97%)
  between operations  1.28 us (3%)
    pallas_call x1, Pallas kernels, on_device(): pl.pallas_call(functools.partial(lambda l, s, e, t, w, o, z, *rest: kerne...  43.4 us
    pallas_call x1, Pallas kernels, on_device(): pl.pallas_call(hand_over, out_shape=(jax.ShapeDtypeStruct((1,), jnp.float...  1.29 us

profile of v5, /device:TPU:1, one launch (start us, length us, event | category | flops | bytes accessed | tf_op | source)
XLA Modules:
  0.0 45.9 jit_solution(9330112658997183361)
XLA Ops:
  1.3 43.4 %crps_exchange.1 = (f32[1,128]{1,0:T(1,128)S(1)}, bf16[8,9,8,1440]{3,2,1,0:T(8,128)(2,1)S(1)}) custom-call(bf16[8,9,8,1440]{3,2,1,0:T(8,128)(2,1)} %bitcast.6, bf16[9,8,1440]{2,1,0:T(8,128)(2,1)} %bitcast.7, f32[1]{0:T(128)S(6)} %copy.6.w), custom_call_target="tpu_custom_call" | custom-call | tf_op jit(solution)/shard_map/crps_exchange/pallas_call | solution.py:353
  44.7 1.3 %hand_over.1 = (f32[1]{0:T(128)}, bf16[8,9,8,1440]{3,2,1,0:T(8,128)(2,1)}) custom-call(f32[1,128]{1,0:T(1,128)S(1)} %get-tuple-element.6.loss, bf16[8,9,8,1440]{3,2,1,0:T(8,128)(2,1)S(1)} %get-tuple-element.7.grads), custom_call_target="tpu_custom_call" | custom-call | tf_op jit(solution)/shard_map/hand_over/pallas_call | solution.py:408
